TPU v7x, 32 devices: a whole 2x2x4 slice. The times are simulated.
32 devices in a mesh: row: 8 (over z, x), col: 4 (over y, core).
Axes of the slice: x: 2, y: 2, z: 4, core: 2. Of those that a mesh axis runs over, the one named last changes fastest.
Arguments:
- src_points: float32 [64, 8192], P(None, ('row', 'col')), as said below
- tgt_points: float32 [64, 16384], P(None, ('col', 'row')), as said below
- log_a: float32 [8192], P('row'), may hold values from -5 to 5
- log_b: float32 [16384], P('col'), may hold values from -5 to 5
- g_current: float32 [16384], P(('col', 'row')), may hold values from -4 to 4
- hist_g: float32 [4, 16384], P(None, ('col', 'row')), may hold values from -4 to 4
- hist_maps: float32 [4, 16384], P(None, ('col', 'row')), may hold values from -4 to 4
Outputs:
- f_out: float32 [8192], P('row')
- g_out: float32 [16384], P(('col', 'row'))
Inputs may be any that keep to these rules, and one draw needn't show every extreme that they name: `src_points`: coordinates of the source points. `tgt_points`: coordinates of the target points.
All inputs are finite; a program needn't handle non-finite values.
Results may differ from a plain program's by a relative error of at most 0.0003.
Values sent between devices are 32-bit elements; how exact they have to be, the bound alone decides.
A program may use at most 64 MiB of HBM per device.

v0:
```python
import functools
import math

import jax
import jax.numpy as jnp
from jax import lax
from jax.experimental import pallas as pl
from jax.experimental.pallas import tpu as pltpu
from jax.sharding import PartitionSpec as P

MESH = pl.DeviceIdType.MESH
HIST = 5
ITERS = 2
EPS = 0.1
LOG2E = math.log2(math.e)
INV = LOG2E / EPS
BACK = EPS * math.log(2.0)
LANES = 128
F32 = jnp.float32
BF16 = jnp.bfloat16


def rounded(value):
    return value.astype(BF16).astype(F32)


def split3(value):
    first = rounded(value)
    second = rounded(value - first)
    return first, second, rounded(value - first - second)


def select_rows(shape, rows):
    at = lax.broadcasted_iota(jnp.int32, shape, 0)
    out = jnp.zeros(shape, F32)
    for index, row in rows:
        out = jnp.where(at == index, row, out)
    return out


def solve_small(rows_list, values):
    extent = len(values)
    rows_list = [list(row) for row in rows_list]
    values = list(values)
    for pivot in range(extent):
        for lower in range(pivot + 1, extent):
            factor = rows_list[lower][pivot] / rows_list[pivot][pivot]
            for at in range(pivot, extent):
                rows_list[lower][at] = rows_list[lower][at] - factor * rows_list[pivot][at]
            values[lower] = values[lower] - factor * values[pivot]
    answer = [None] * extent
    for pivot in reversed(range(extent)):
        running = values[pivot]
        for upper in range(pivot + 1, extent):
            running = running - rows_list[pivot][upper] * answer[upper]
        answer[pivot] = running / rows_list[pivot][pivot]
    return answer


def kernel(
    R, C,
    src_ref, tgt_ref, la_ref, lb_ref, g_ref, hg_ref, hm_ref,
    f_ref, gout_ref,
    src_all, tgt_all, g_all, hm_all, xt, xlow, y_all, ysq, mrow, srow,
    rp_send, rp_all, cp_send, cp_all, mp_send, mp_all, gc_send, gc_all,
    s_src, r_src, s_tgt, r_tgt, s_g, r_g, s_hm, r_hm,
    s_rp, r_rp, s_cp, r_cp, s_mp, r_mp, s_gc, r_gc,
):
    row = lax.axis_index("row")
    col = lax.axis_index("col")
    depth, nsrc = src_ref.shape
    ntgt = tgt_ref.shape[1]
    nrow = C * nsrc
    kdim = 4 * depth
    itile = min(256, nrow)
    pending = []

    def to_row(k):
        return lax.rem(row + k, R)

    def to_col(k):
        return lax.rem(col + k, C)

    def send(src, dst, ssem, rsem, device):
        copy = pltpu.make_async_remote_copy(
            src_ref=src, dst_ref=dst, send_sem=ssem, recv_sem=rsem,
            device_id=device, device_id_type=MESH,
        )
        copy.start()
        pending.append(copy)

    def arrived(dst, ssem, rsem):
        pltpu.make_async_remote_copy(
            src_ref=dst, dst_ref=dst, send_sem=ssem, recv_sem=rsem,
            device_id=(row, col), device_id_type=MESH,
        ).wait_recv()

    for k in range(1, C):
        p = to_col(k)
        send(src_ref, src_all.at[col], s_src.at[p], r_src.at[col], (row, p))
    for k in range(1, R):
        p = to_row(k)
        send(g_ref, g_all.at[row], s_g.at[p], r_g.at[row], (p, col))
        send(tgt_ref, tgt_all.at[row], s_tgt.at[p], r_tgt.at[row], (p, col))
    for k in range(1, R):
        p = to_row(k)
        send(hm_ref, hm_all.at[row], s_hm.at[p], r_hm.at[row], (p, col))

    src_all[col] = src_ref[...]
    tgt_all[row] = tgt_ref[...]
    g_all[row] = g_ref[...]
    hm_all[row] = hm_ref[...]

    def build_x(c):
        x = src_all[c]
        scaled = x * (2.0 * INV)
        high = rounded(scaled)
        low = rounded(scaled - high)
        ones = select_rows((depth, nsrc), [(k, 1.0) for k in range(3)])
        whole = jnp.concatenate([high, high, low, ones], axis=0).T.astype(BF16)
        at = pl.ds(pl.multiple_of(c * nsrc, nsrc), nsrc)
        xt[0, at, :] = whole
        xt[1, at, :] = whole
        xlow[c] = low
        return jnp.sum(x * x, axis=0, keepdims=True)

    def bias_y(p, g):
        bias = INV * g + LOG2E * lb_ref[pl.ds(p, 1), :] - INV * ysq[p]
        b1, b2, b3 = split3(bias)
        rows = [(0, b1), (1, b2), (2, b3)] + [(k, 1.0) for k in range(3, 6)]
        y_all[p, 3 * depth : 3 * depth + 16, :] = select_rows((16, ntgt), rows).astype(BF16)

    def build_y(p):
        y = tgt_all[p]
        high = y.astype(BF16)
        low = (y - high.astype(F32)).astype(BF16)
        y_all[p, 0:depth, :] = high
        y_all[p, depth : 2 * depth, :] = low
        y_all[p, 2 * depth : 3 * depth, :] = high
        y_all[p, 3 * depth + 16 :, :] = jnp.zeros((depth - 16, ntgt), BF16)
        ysq[p] = jnp.sum(y * y, axis=0, keepdims=True)
        bias_y(p, g_all[p])

    def row_chunk(p):
        for it in range(nrow // itile):
            at = slice(it * itile, (it + 1) * itile)
            s = jnp.dot(xt[0, at, :], y_all[p], preferred_element_type=F32)
            pieces = [s[:, k : k + LANES] for k in range(0, ntgt, LANES)]
            old = mrow[at, :]
            top = functools.reduce(jnp.maximum, pieces, old)
            total = srow[at, :] * jnp.exp2(old - top)
            for piece in pieces:
                total = total + jnp.exp2(piece - top)
            mrow[at, :] = top
            srow[at, :] = total

    def row_finish(turn):
        for at in range(0, nrow, LANES):
            mt = mrow[at : at + LANES, :].T
            st = srow[at : at + LANES, :].T
            top = jnp.max(mt, axis=0, keepdims=True)
            total = jnp.sum(st * jnp.exp2(mt - top), axis=0, keepdims=True)
            rp_send[turn, 0:1, at : at + LANES] = top
            rp_send[turn, 1:2, at : at + LANES] = total
        for k in range(1, C):
            p = to_col(k)
            send(rp_send.at[turn], rp_all.at[turn, col], s_rp.at[turn, p], r_rp.at[turn, col], (row, p))
        rp_all[turn, col] = rp_send[turn]
        for k in range(1, C):
            p = to_col(k)
            arrived(rp_all.at[turn, p], s_rp.at[turn, p], r_rp.at[turn, p])
        tops = [rp_all[turn, c, 0:1, :] for c in range(C)]
        top = functools.reduce(jnp.maximum, tops)
        total = jnp.zeros_like(top)
        for c in range(C):
            total = total + rp_all[turn, c, 1:2, :] * jnp.exp2(tops[c] - top)
        return top + jnp.log2(total)

    def set_row_term(lse):
        a1, a2, a3 = split3(LOG2E * la_ref[...] - lse)
        for c in range(C):
            at = slice(c * nsrc, (c + 1) * nsrc)
            rows = [(3, a1[:, at]), (4, a2[:, at]), (5, a3[:, at])]
            slab = jnp.concatenate([xlow[c], select_rows((depth, nsrc), rows)], axis=0)
            xt[1, at, 2 * depth :] = slab.T.astype(BF16)

    def col_chunk(turn, p):
        top = jnp.full((8, ntgt), -jnp.inf, F32)
        total = jnp.zeros((8, ntgt), F32)
        for it in range(nrow // itile):
            at = slice(it * itile, (it + 1) * itile)
            s = jnp.dot(xt[1, at, :], y_all[p], preferred_element_type=F32)
            s = s.reshape(itile // 8, 8, ntgt)
            new = jnp.maximum(top, jnp.max(s, axis=0))
            total = total * jnp.exp2(top - new) + jnp.sum(jnp.exp2(s - new[None]), axis=0)
            top = new
        best = jnp.max(top, axis=0, keepdims=True)
        cp_send[turn, p, 0:1, :] = best
        cp_send[turn, p, 1:2, :] = jnp.sum(total * jnp.exp2(top - best), axis=0, keepdims=True)

    def zero_bias(p, carry):
        at = lax.broadcasted_iota(jnp.int32, (16, ntgt), 0)
        one = jnp.where((at >= 3) & (at < 6), 1.0, 0.0)
        y_all[p, 3 * depth : 3 * depth + 16, :] = one.astype(BF16)
        return carry

    def reset_rows():
        mrow[...] = jnp.full(mrow.shape, -jnp.inf, F32)
        srow[...] = jnp.zeros(srow.shape, F32)

    reset_rows()
    for k in range(1, C):
        p = to_col(k)
        arrived(src_all.at[p], s_src.at[p], r_src.at[p])
    xsq = jnp.concatenate([build_x(c) for c in range(C)], axis=1)

    potentials = [hg_ref[k : k + 1, :] for k in range(hg_ref.shape[0])]
    images = [hm_ref[k : k + 1, :] for k in range(hm_ref.shape[0])]
    g_share = g_ref[...]
    own = tgt_ref[...]
    own_sq = jnp.sum(own * own, axis=0, keepdims=True)
    pairs = [(i, j) for i in range(HIST) for j in range(i, HIST)]
    grows = -(-len(pairs) // 8) * 8
    for turn in range(ITERS):
        if turn == 0:
            build_y(row)
            row_chunk(row)

            def first(k, carry):
                p = lax.rem(row + k, R)
                arrived(g_all.at[p], s_g.at[p], r_g.at[p])
                arrived(tgt_all.at[p], s_tgt.at[p], r_tgt.at[p])
                build_y(p)
                row_chunk(p)
                return carry

            lax.fori_loop(1, R, first, 0)
        else:
            reset_rows()

            def again(p, carry):
                row_chunk(p)
                return carry

            lax.fori_loop(0, R, again, 0)
        lse = row_finish(turn)
        if turn == ITERS - 1:
            f_ref[...] = xsq - BACK * lse
        set_row_term(lse)
        lax.fori_loop(0, R, zero_bias, 0)

        def cols(k, carry):
            p = lax.rem(row + k, R)
            col_chunk(turn, p)
            pltpu.make_async_remote_copy(
                src_ref=cp_send.at[turn, p], dst_ref=cp_all.at[turn, row],
                send_sem=s_cp.at[turn, p], recv_sem=r_cp.at[turn, row],
                device_id=(p, col), device_id_type=MESH,
            ).start()
            return carry

        lax.fori_loop(1, R, cols, 0)
        col_chunk(turn, row)
        cp_all[turn, row] = cp_send[turn, row]
        for k in range(1, R):
            p = to_row(k)
            arrived(cp_all.at[turn, p], s_cp.at[turn, p], r_cp.at[turn, p])
        tops = [cp_all[turn, p, 0:1, :] for p in range(R)]
        best = functools.reduce(jnp.maximum, tops)
        total = jnp.zeros_like(best)
        for p in range(R):
            total = total + cp_all[turn, p, 1:2, :] * jnp.exp2(tops[p] - best)
        mapped = own_sq - BACK * (best + jnp.log2(total))
        potentials = (potentials + [g_share])[-HIST:]
        images = (images + [mapped])[-HIST:]
        resid = [a - b for a, b in zip(images, potentials)]
        for at, (i, j) in enumerate(pairs):
            product = resid[i] * resid[j]
            mp_send[turn, at : at + 1, :] = sum(product[:, k : k + LANES] for k in range(0, ntgt, LANES))
        for at in range(len(pairs), grows):
            mp_send[turn, at : at + 1, :] = jnp.zeros((1, LANES), F32)
        for at in range(ntgt // LANES):
            mp_send[turn, grows + at : grows + at + 1, :] = mapped[:, at * LANES : (at + 1) * LANES]
        for k in range(1, R):
            p = to_row(k)
            send(mp_send.at[turn], mp_all.at[turn, row], s_mp.at[turn, p], r_mp.at[turn, row], (p, col))
        mp_all[turn, row] = mp_send[turn]
        for k in range(1, R):
            p = to_row(k)
            arrived(mp_all.at[turn, p], s_mp.at[turn, p], r_mp.at[turn, p])
        gram = mp_all[turn, 0, 0:grows, :]
        for p in range(1, R):
            gram = gram + mp_all[turn, p, 0:grows, :]
        gc_send[turn] = gram
        for k in range(1, C):
            p = to_col(k)
            send(gc_send.at[turn], gc_all.at[turn, col], s_gc.at[turn, p], r_gc.at[turn, col], (row, p))
        gc_all[turn, col] = gram
        for k in range(1, C):
            p = to_col(k)
            arrived(gc_all.at[turn, p], s_gc.at[turn, p], r_gc.at[turn, p])
        gram = gc_all[turn, 0]
        for c in range(1, C):
            gram = gram + gc_all[turn, c]
        gram = jnp.broadcast_to(jnp.sum(gram, axis=1, keepdims=True), (grows, LANES))
        system = [[None] * HIST for _ in range(HIST)]
        for at, (i, j) in enumerate(pairs):
            system[i][j] = system[j][i] = gram[at : at + 1, :]
        trace = functools.reduce(jnp.add, [system[i][i] for i in range(HIST)])
        shift = 0.001 * trace / HIST + 1e-06
        for i in range(HIST):
            system[i][i] = system[i][i] + shift
        weights = solve_small(system, [jnp.ones((1, LANES), F32)] * HIST)
        norm = functools.reduce(jnp.add, weights)
        mix = [jnp.concatenate([w / norm] * (ntgt // LANES), axis=1) for w in weights]

        def mixed(parts):
            return functools.reduce(jnp.add, [w * part for w, part in zip(mix, parts)])

        g_share = mixed(images)
        if turn < ITERS - 1:
            if turn == 0:
                for k in range(1, R):
                    p = to_row(k)
                    arrived(hm_all.at[p], s_hm.at[p], r_hm.at[p])
            for p in range(R):
                known = [hm_all[p, k : k + 1, :] for k in range(hm_ref.shape[0])]
                for past in range(turn + 1):
                    rows = [mp_all[past, p, grows + at : grows + at + 1, :] for at in range(ntgt // LANES)]
                    known.append(jnp.concatenate(rows, axis=1))
                bias_y(p, mixed(known[-HIST:]))
    gout_ref[...] = g_share
    for copy in pending:
        copy.wait_send()
    for turn in range(ITERS):
        for k in range(1, R):
            p = to_row(k)
            pltpu.make_async_remote_copy(
                src_ref=cp_send.at[turn, p], dst_ref=cp_all.at[turn, row],
                send_sem=s_cp.at[turn, p], recv_sem=r_cp.at[turn, row],
                device_id=(p, col), device_id_type=MESH,
            ).wait_send()


def shards(R, C, src, tgt, log_a, log_b, g_current, hist_g, hist_maps):
    depth, nsrc = src.shape
    ntgt = tgt.shape[1]
    nrow = C * nsrc
    nhist = hist_g.shape[0]
    pair_rows = -(-(HIST * (HIST + 1) // 2) // 8) * 8
    mp_rows = -(-(pair_rows + ntgt // LANES) // 8) * 8
    dma = pltpu.SemaphoreType.DMA
    vmem = pl.BlockSpec(memory_space=pltpu.VMEM)
    f_out, g_out = pl.pallas_call(
        functools.partial(kernel, R, C),
        out_shape=(
            jax.ShapeDtypeStruct((1, nrow), F32),
            jax.ShapeDtypeStruct((1, ntgt), F32),
        ),
        in_specs=[vmem] * 7,
        out_specs=(vmem, vmem),
        scratch_shapes=[
            pltpu.VMEM((C, depth, nsrc), F32),
            pltpu.VMEM((R, depth, ntgt), F32),
            pltpu.VMEM((R, 1, ntgt), F32),
            pltpu.VMEM((R, nhist, ntgt), F32),
            pltpu.VMEM((2, nrow, 4 * depth), BF16),
            pltpu.VMEM((C, depth, nsrc), F32),
            pltpu.VMEM((R, 4 * depth, ntgt), BF16),
            pltpu.VMEM((R, 1, ntgt), F32),
            pltpu.VMEM((nrow, LANES), F32),
            pltpu.VMEM((nrow, LANES), F32),
            pltpu.VMEM((ITERS, 2, nrow), F32),
            pltpu.VMEM((ITERS, C, 2, nrow), F32),
            pltpu.VMEM((ITERS, R, 2, ntgt), F32),
            pltpu.VMEM((ITERS, R, 2, ntgt), F32),
            pltpu.VMEM((ITERS, mp_rows, LANES), F32),
            pltpu.VMEM((ITERS, R, mp_rows, LANES), F32),
            pltpu.VMEM((ITERS, pair_rows, LANES), F32),
            pltpu.VMEM((ITERS, C, pair_rows, LANES), F32),
            dma((C,)), dma((C,)), dma((R,)), dma((R,)),
            dma((R,)), dma((R,)), dma((R,)), dma((R,)),
            dma((ITERS, C)), dma((ITERS, C)), dma((ITERS, R)), dma((ITERS, R)),
            dma((ITERS, R)), dma((ITERS, R)), dma((ITERS, C)), dma((ITERS, C)),
        ],
        compiler_params=pltpu.CompilerParams(
            has_side_effects=True, vmem_limit_bytes=48 * 1024 * 1024
        ),
    )(
        src, tgt, log_a.reshape(1, nrow), log_b.reshape(R, ntgt),
        g_current.reshape(1, ntgt), hist_g, hist_maps,
    )
    return f_out.reshape(nrow), g_out.reshape(ntgt)


def solution(mesh):
    in_specs = (
        P(None, ("row", "col")),
        P(None, ("col", "row")),
        P("row"),
        P("col"),
        P(("col", "row")),
        P(None, ("col", "row")),
        P(None, ("col", "row")),
    )
    out_specs = (P("row"), P(("col", "row")))
    body = functools.partial(shards, mesh.shape["row"], mesh.shape["col"])
    return jax.shard_map(body, mesh=mesh, in_specs=in_specs, out_specs=out_specs, check_vma=False)
```

profile of v0, /device:TPU:0, one launch (start us, length us, event | category | flops | bytes accessed | tf_op | source)
XLA Modules:
  0.0 83.6 jit_solution(3927939265426932258)
XLA Ops:
  0.6 0.0 copy-start.2
  0.6 0.0 copy-start.3
  0.7 0.0 copy-start.4
  0.7 0.0 copy-start.5
  0.7 0.7 reshape.20.lb_ref
  1.4 0.0 copy-done.2
  1.4 0.0 copy-done.3
  1.4 0.0 copy-done.4
  1.4 0.0 copy-done.5
  1.4 0.0 copy-start
  1.4 0.9 %copy-done = f32[64,512]{1,0:T(8,128)S(1)} copy-done((f32[64,512]{1,0:T(8,128)S(1)}, f32[64,512]{1,0:T(8,128)}, u32[]{:S(2)}) %copy-start) | copy-done | bytes 131096
  2.3 0.0 copy-start.1
  2.3 0.8 %copy-done.1 = f32[64,256]{1,0:T(8,128)S(1)} copy-done((f32[64,256]{1,0:T(8,128)S(1)}, f32[64,256]{1,0:T(8,128)}, u32[]{:S(2)}) %copy-start.1) | copy-done | bytes 65560
  3.2 79.2 %shard_map.86 = (f32[1,1024]{1,0:T(1,128)S(1)}, f32[1,512]{1,0:T(1,128)S(1)}) custom-call(f32[64,256]{1,0:T(8,128)S(1)} %copy-done.1, f32[64,512]{1,0:T(8,128)S(1)} %copy-done, f32[1,1024]{1,0:T(1,128)S(1)} %bitcast.4, f32[8,512]{1,0:T(8,128)S(1)} %reshape.20.lb_ref, f32[1,512]{1,0:T(1,128)S(1)} %bitcast.6, f32[4,512]{1,0:T(4,128)S(1)} %copy-done.2, ...), custom_call_target="tpu_custom_call" | custom-call | tf_op jit(solution)/shard_map/pallas_call | solution.py:354
  82.4 0.6 copy.11
  83.0 0.6 copy.12
Async XLA Ops:
  0.6 0.8 copy-start.2
  0.6 0.8 copy-start.3
  0.7 0.8 copy-start.4
  0.7 0.8 copy-start.5
  1.4 0.9 %copy-start = (f32[64,512]{1,0:T(8,128)S(1)}, f32[64,512]{1,0:T(8,128)}, u32[]{:S(2)}) copy-start(f32[64,512]{1,0:T(8,128)} %tgt_ref.1) | copy-start | bytes 393220
  2.3 0.8 %copy-start.1 = (f32[64,256]{1,0:T(8,128)S(1)}, f32[64,256]{1,0:T(8,128)}, u32[]{:S(2)}) copy-start(f32[64,256]{1,0:T(8,128)} %src_ref.1) | copy-start | bytes 196612
where the time goes:
time: 83.9 us; the launch traced here: 83.6 us
  Pallas kernels  79.2 us (94%)
  local copies, waits for them, and re-layouts  3.67 us (4%)
    pallas_call x1, Pallas kernels, shards(): pl.pallas_call(functools.partial(kernel, R, C), out_shape=(jax.ShapeDtype...  79.2 us
    unnamed x14, local copies, waits for them, and re-layouts  2.93 us

commit v1 on v0

--- a/solution.py
+++ b/solution.py
@@ -57,6 +57,13 @@
     return answer
 
 
+def inner_extent(R):
+    best = 1
+    while best * best * 4 <= R and R % (best * 2) == 0:
+        best *= 2
+    return best
+
+
 def kernel(
     R, C,
     src_ref, tgt_ref, la_ref, lb_ref, g_ref, hg_ref, hm_ref,
@@ -81,6 +88,13 @@
     def to_col(k):
         return lax.rem(col + k, C)
 
+    X = inner_extent(R)
+    Z = R // X
+    outer, inner = row // X, lax.rem(row, X)
+
+    def place(k, m):
+        return lax.rem(outer + k, Z) * X + lax.rem(inner + m, X)
+
     def send(src, dst, ssem, rsem, device):
         copy = pltpu.make_async_remote_copy(
             src_ref=src, dst_ref=dst, send_sem=ssem, recv_sem=rsem,
@@ -101,6 +115,11 @@
     for k in range(1, R):
         p = to_row(k)
         send(g_ref, g_all.at[row], s_g.at[p], r_g.at[row], (p, col))
+    for k in range(1, Z):
+        p = place(k, 0)
+        send(tgt_ref, tgt_all.at[row], s_tgt.at[p], r_tgt.at[row], (p, col))
+    for k in range(1, X):
+        p = place(0, k)
         send(tgt_ref, tgt_all.at[row], s_tgt.at[p], r_tgt.at[row], (p, col))
     for k in range(1, R):
         p = to_row(k)
@@ -226,15 +245,40 @@
             build_y(row)
             row_chunk(row)
 
-            def first(k, carry):
-                p = lax.rem(row + k, R)
+            def take(p):
                 arrived(g_all.at[p], s_g.at[p], r_g.at[p])
-                arrived(tgt_all.at[p], s_tgt.at[p], r_tgt.at[p])
                 build_y(p)
                 row_chunk(p)
+
+            def passed_on(p, q):
+                return pltpu.make_async_remote_copy(
+                    src_ref=tgt_all.at[p], dst_ref=tgt_all.at[p],
+                    send_sem=s_tgt.at[q], recv_sem=r_tgt.at[p],
+                    device_id=(row - inner + lax.rem(q, X), col),
+                    device_id_type=MESH,
+                )
+
+            def first(k, carry):
+                p = place(k, 0)
+                arrived(tgt_all.at[p], s_tgt.at[p], r_tgt.at[p])
+                for m in range(1, X):
+                    passed_on(p, place(k, m)).start()
+                take(p)
                 return carry
 
-            lax.fori_loop(1, R, first, 0)
+            lax.fori_loop(1, Z, first, 0)
+
+            def rest(n, carry):
+                p = place(n // (X - 1), 1 + lax.rem(n, X - 1))
+                arrived(tgt_all.at[p], s_tgt.at[p], r_tgt.at[p])
+                take(p)
+                return carry
+
+            if X > 1:
+                lax.fori_loop(0, Z * (X - 1), rest, 0)
+            for k in range(1, Z):
+                for m in range(1, X):
+                    passed_on(place(k, 0), place(k, m)).wait_send()
         else:
             reset_rows()
 

time: 83.9 us -> 79.4 us (0.946)
  Pallas kernels: 79.2 us -> 74.7 us
    pallas_call x1, Pallas kernels: 79.2 us -> 74.7 us  [shards(): pl.pallas_call(functools.partial(kernel, R, C), out_shape=(jax.ShapeDtype...]
where the time goes in v1:
time: 79.4 us; the launch traced here: 79.1 us
  Pallas kernels  74.7 us (94%)
  local copies, waits for them, and re-layouts  3.67 us (5%)
    pallas_call x1, Pallas kernels, shards(): pl.pallas_call(functools.partial(kernel, R, C), out_shape=(jax.ShapeDtype...  74.7 us
    unnamed x14, local copies, waits for them, and re-layouts  2.93 us

profile of v1, /device:TPU:0, one launch (start us, length us, event | category | flops | bytes accessed | tf_op | source)
XLA Modules:
  0.0 79.1 jit_solution(15970013078239550304)
XLA Ops:
  0.6 0.0 copy-start.2
  0.6 0.0 copy-start.3
  0.7 0.0 copy-start.4
  0.7 0.0 copy-start.5
  0.7 0.7 reshape.20.lb_ref
  1.4 0.0 copy-done.2
  1.4 0.0 copy-done.3
  1.4 0.0 copy-done.4
  1.4 0.0 copy-done.5
  1.4 0.0 copy-start
  1.4 0.9 %copy-done = f32[64,512]{1,0:T(8,128)S(1)} copy-done((f32[64,512]{1,0:T(8,128)S(1)}, f32[64,512]{1,0:T(8,128)}, u32[]{:S(2)}) %copy-start) | copy-done | bytes 131096
  2.3 0.0 copy-start.1
  2.3 0.8 %copy-done.1 = f32[64,256]{1,0:T(8,128)S(1)} copy-done((f32[64,256]{1,0:T(8,128)S(1)}, f32[64,256]{1,0:T(8,128)}, u32[]{:S(2)}) %copy-start.1) | copy-done | bytes 65560
  3.2 74.7 %shard_map.86 = (f32[1,1024]{1,0:T(1,128)S(1)}, f32[1,512]{1,0:T(1,128)S(1)}) custom-call(f32[64,256]{1,0:T(8,128)S(1)} %copy-done.1, f32[64,512]{1,0:T(8,128)S(1)} %copy-done, f32[1,1024]{1,0:T(1,128)S(1)} %bitcast.4, f32[8,512]{1,0:T(8,128)S(1)} %reshape.20.lb_ref, f32[1,512]{1,0:T(1,128)S(1)} %bitcast.6, f32[4,512]{1,0:T(4,128)S(1)} %copy-done.2, ...), custom_call_target="tpu_custom_call" | custom-call | tf_op jit(solution)/shard_map/pallas_call | solution.py:398
  77.9 0.6 copy.11
  78.5 0.6 copy.12
Async XLA Ops:
  0.6 0.8 copy-start.2
  0.6 0.8 copy-start.3
  0.7 0.8 copy-start.4
  0.7 0.8 copy-start.5
  1.4 0.9 %copy-start = (f32[64,512]{1,0:T(8,128)S(1)}, f32[64,512]{1,0:T(8,128)}, u32[]{:S(2)}) copy-start(f32[64,512]{1,0:T(8,128)} %tgt_ref.1) | copy-start | bytes 393220
  2.3 0.8 %copy-start.1 = (f32[64,256]{1,0:T(8,128)S(1)}, f32[64,256]{1,0:T(8,128)}, u32[]{:S(2)}) copy-start(f32[64,256]{1,0:T(8,128)} %src_ref.1) | copy-start | bytes 196612

commit v2 on v1

--- a/solution.py
+++ b/solution.py
@@ -69,9 +69,9 @@
     src_ref, tgt_ref, la_ref, lb_ref, g_ref, hg_ref, hm_ref,
     f_ref, gout_ref,
     src_all, tgt_all, g_all, hm_all, xt, xlow, y_all, ysq, mrow, srow,
-    rp_send, rp_all, cp_send, cp_all, mp_send, mp_all, gc_send, gc_all,
+    rp_send, rp_all, cp_send, cp_all, mp_send, mp_all, ga_send, ga_all,
     s_src, r_src, s_tgt, r_tgt, s_g, r_g, s_hm, r_hm,
-    s_rp, r_rp, s_cp, r_cp, s_mp, r_mp, s_gc, r_gc,
+    s_rp, r_rp, s_cp, r_cp, s_mp, r_mp, s_ga, r_ga,
 ):
     row = lax.axis_index("row")
     col = lax.axis_index("col")
@@ -318,35 +318,51 @@
         potentials = (potentials + [g_share])[-HIST:]
         images = (images + [mapped])[-HIST:]
         resid = [a - b for a, b in zip(images, potentials)]
+        lanes = lax.broadcasted_iota(jnp.int32, (1, LANES), 1)
+        share = jnp.zeros((1, LANES), F32)
         for at, (i, j) in enumerate(pairs):
-            product = resid[i] * resid[j]
-            mp_send[turn, at : at + 1, :] = sum(product[:, k : k + LANES] for k in range(0, ntgt, LANES))
-        for at in range(len(pairs), grows):
-            mp_send[turn, at : at + 1, :] = jnp.zeros((1, LANES), F32)
-        for at in range(ntgt // LANES):
-            mp_send[turn, grows + at : grows + at + 1, :] = mapped[:, at * LANES : (at + 1) * LANES]
-        for k in range(1, R):
-            p = to_row(k)
-            send(mp_send.at[turn], mp_all.at[turn, row], s_mp.at[turn, p], r_mp.at[turn, row], (p, col))
-        mp_all[turn, row] = mp_send[turn]
-        for k in range(1, R):
-            p = to_row(k)
-            arrived(mp_all.at[turn, p], s_mp.at[turn, p], r_mp.at[turn, p])
-        gram = mp_all[turn, 0, 0:grows, :]
-        for p in range(1, R):
-            gram = gram + mp_all[turn, p, 0:grows, :]
-        gc_send[turn] = gram
-        for k in range(1, C):
-            p = to_col(k)
-            send(gc_send.at[turn], gc_all.at[turn, col], s_gc.at[turn, p], r_gc.at[turn, col], (row, p))
-        gc_all[turn, col] = gram
-        for k in range(1, C):
-            p = to_col(k)
-            arrived(gc_all.at[turn, p], s_gc.at[turn, p], r_gc.at[turn, p])
-        gram = gc_all[turn, 0]
-        for c in range(1, C):
-            gram = gram + gc_all[turn, c]
-        gram = jnp.broadcast_to(jnp.sum(gram, axis=1, keepdims=True), (grows, LANES))
+            share = jnp.where(lanes == at, jnp.sum(resid[i] * resid[j], axis=1, keepdims=True), share)
+        ga_send[turn] = share
+        me = row * C + col
+
+        def gram_copy(n):
+            d = lax.rem(me + n, R * C)
+            return pltpu.make_async_remote_copy(
+                src_ref=ga_send.at[turn], dst_ref=ga_all.at[turn, me],
+                send_sem=s_ga.at[turn, d], recv_sem=r_ga.at[turn, me],
+                device_id=(d // C, lax.rem(d, C)), device_id_type=MESH,
+            )
+
+        def gram_out(n, carry):
+            gram_copy(n).start()
+            return carry
+
+        def gram_in(n, carry):
+            d = lax.rem(me + n, R * C)
+            arrived(ga_all.at[turn, d], s_ga.at[turn, d], r_ga.at[turn, d])
+            return carry
+
+        def gram_done(n, carry):
+            gram_copy(n).wait_send()
+            return carry
+
+        lax.fori_loop(1, R * C, gram_out, 0)
+        if turn < ITERS - 1:
+            mp_send[turn] = mapped
+            for k in range(1, R):
+                p = to_row(k)
+                send(mp_send.at[turn], mp_all.at[turn, row], s_mp.at[turn, p], r_mp.at[turn, row], (p, col))
+            mp_all[turn, row] = mapped
+        ga_all[turn, me] = share
+        lax.fori_loop(1, R * C, gram_in, 0)
+        gram = jnp.sum(ga_all[turn], axis=0)
+        lax.fori_loop(1, R * C, gram_done, 0)
+        wide = jnp.broadcast_to(gram, (grows, LANES))
+        picked = lax.broadcasted_iota(jnp.int32, (grows, LANES), 0) == lax.broadcasted_iota(
+            jnp.int32, (grows, LANES), 1
+        )
+        gram = jnp.sum(jnp.where(picked, wide, 0.0), axis=1, keepdims=True)
+        gram = jnp.broadcast_to(gram, (grows, LANES))
         system = [[None] * HIST for _ in range(HIST)]
         for at, (i, j) in enumerate(pairs):
             system[i][j] = system[j][i] = gram[at : at + 1, :]
@@ -367,11 +383,13 @@
                 for k in range(1, R):
                     p = to_row(k)
                     arrived(hm_all.at[p], s_hm.at[p], r_hm.at[p])
+            for k in range(1, R):
+                p = to_row(k)
+                arrived(mp_all.at[turn, p], s_mp.at[turn, p], r_mp.at[turn, p])
             for p in range(R):
                 known = [hm_all[p, k : k + 1, :] for k in range(hm_ref.shape[0])]
                 for past in range(turn + 1):
-                    rows = [mp_all[past, p, grows + at : grows + at + 1, :] for at in range(ntgt // LANES)]
-                    known.append(jnp.concatenate(rows, axis=1))
+                    known.append(mp_all[past, p])
                 bias_y(p, mixed(known[-HIST:]))
     gout_ref[...] = g_share
     for copy in pending:
@@ -391,8 +409,6 @@
     ntgt = tgt.shape[1]
     nrow = C * nsrc
     nhist = hist_g.shape[0]
-    pair_rows = -(-(HIST * (HIST + 1) // 2) // 8) * 8
-    mp_rows = -(-(pair_rows + ntgt // LANES) // 8) * 8
     dma = pltpu.SemaphoreType.DMA
     vmem = pl.BlockSpec(memory_space=pltpu.VMEM)
     f_out, g_out = pl.pallas_call(
@@ -418,14 +434,14 @@
             pltpu.VMEM((ITERS, C, 2, nrow), F32),
             pltpu.VMEM((ITERS, R, 2, ntgt), F32),
             pltpu.VMEM((ITERS, R, 2, ntgt), F32),
-            pltpu.VMEM((ITERS, mp_rows, LANES), F32),
-            pltpu.VMEM((ITERS, R, mp_rows, LANES), F32),
-            pltpu.VMEM((ITERS, pair_rows, LANES), F32),
-            pltpu.VMEM((ITERS, C, pair_rows, LANES), F32),
+            pltpu.VMEM((ITERS, 1, ntgt), F32),
+            pltpu.VMEM((ITERS, R, 1, ntgt), F32),
+            pltpu.VMEM((ITERS, 1, LANES), F32),
+            pltpu.VMEM((ITERS, R * C, 1, LANES), F32),
             dma((C,)), dma((C,)), dma((R,)), dma((R,)),
             dma((R,)), dma((R,)), dma((R,)), dma((R,)),
             dma((ITERS, C)), dma((ITERS, C)), dma((ITERS, R)), dma((ITERS, R)),
-            dma((ITERS, R)), dma((ITERS, R)), dma((ITERS, C)), dma((ITERS, C)),
+            dma((ITERS, R)), dma((ITERS, R)), dma((ITERS, R * C)), dma((ITERS, R * C)),
         ],
         compiler_params=pltpu.CompilerParams(
             has_side_effects=True, vmem_limit_bytes=48 * 1024 * 1024

time: 79.4 us -> 77 us (0.970)
  Pallas kernels: 74.7 us -> 72.4 us
    pallas_call x1, Pallas kernels: 74.7 us -> 72.4 us  [shards(): pl.pallas_call(functools.partial(kernel, R, C), out_shape=(jax.ShapeDtype...]
where the time goes in v2:
time: 77 us; the launch traced here: 76.8 us
  Pallas kernels  72.4 us (94%)
  local copies, waits for them, and re-layouts  3.67 us (5%)
    pallas_call x1, Pallas kernels, shards(): pl.pallas_call(functools.partial(kernel, R, C), out_shape=(jax.ShapeDtype...  72.4 us
    unnamed x14, local copies, waits for them, and re-layouts  2.93 us

profile of v2, /device:TPU:0, one launch (start us, length us, event | category | flops | bytes accessed | tf_op | source)
XLA Modules:
  0.0 76.8 jit_solution(16860438314192829844)
XLA Ops:
  0.6 0.0 copy-start.2
  0.6 0.0 copy-start.3
  0.7 0.0 copy-start.4
  0.7 0.0 copy-start.5
  0.7 0.7 reshape.20.lb_ref
  1.4 0.0 copy-done.2
  1.4 0.0 copy-done.3
  1.4 0.0 copy-done.4
  1.4 0.0 copy-done.5
  1.4 0.0 copy-start
  1.4 0.9 %copy-done = f32[64,512]{1,0:T(8,128)S(1)} copy-done((f32[64,512]{1,0:T(8,128)S(1)}, f32[64,512]{1,0:T(8,128)}, u32[]{:S(2)}) %copy-start) | copy-done | bytes 131096
  2.3 0.0 copy-start.1
  2.3 0.8 %copy-done.1 = f32[64,256]{1,0:T(8,128)S(1)} copy-done((f32[64,256]{1,0:T(8,128)S(1)}, f32[64,256]{1,0:T(8,128)}, u32[]{:S(2)}) %copy-start.1) | copy-done | bytes 65560
  3.2 72.4 %shard_map.86 = (f32[1,1024]{1,0:T(1,128)S(1)}, f32[1,512]{1,0:T(1,128)S(1)}) custom-call(f32[64,256]{1,0:T(8,128)S(1)} %copy-done.1, f32[64,512]{1,0:T(8,128)S(1)} %copy-done, f32[1,1024]{1,0:T(1,128)S(1)} %bitcast.4, f32[8,512]{1,0:T(8,128)S(1)} %reshape.20.lb_ref, f32[1,512]{1,0:T(1,128)S(1)} %bitcast.6, f32[4,512]{1,0:T(4,128)S(1)} %copy-done.2, ...), custom_call_target="tpu_custom_call" | custom-call | tf_op jit(solution)/shard_map/pallas_call | solution.py:414
  75.6 0.6 copy.11
  76.2 0.6 copy.12
Async XLA Ops:
  0.6 0.8 %copy-start.2 = (f32[4,512]{1,0:T(4,128)S(1)}, f32[4,512]{1,0:T(4,128)}, u32[]{:S(2)}) copy-start(f32[4,512]{1,0:T(4,128)} %hg_ref.1) | copy-start | bytes 24580
  0.6 0.8 %copy-start.3 = (f32[4,512]{1,0:T(4,128)S(1)}, f32[4,512]{1,0:T(4,128)}, u32[]{:S(2)}) copy-start(f32[4,512]{1,0:T(4,128)} %hm_ref.1) | copy-start | bytes 24580
  0.7 0.8 %copy-start.4 = (f32[1024]{0:T(1024)S(1)}, f32[1024]{0:T(1024)}, u32[]{:S(2)}) copy-start(f32[1024]{0:T(1024)} %param.9) | copy-start | bytes 12292
  0.7 0.8 copy-start.5
  1.4 0.9 %copy-start = (f32[64,512]{1,0:T(8,128)S(1)}, f32[64,512]{1,0:T(8,128)}, u32[]{:S(2)}) copy-start(f32[64,512]{1,0:T(8,128)} %tgt_ref.1) | copy-start | bytes 393220
  2.3 0.8 %copy-start.1 = (f32[64,256]{1,0:T(8,128)S(1)}, f32[64,256]{1,0:T(8,128)}, u32[]{:S(2)}) copy-start(f32[64,256]{1,0:T(8,128)} %src_ref.1) | copy-start | bytes 196612

commit v3 on v2

--- a/solution.py
+++ b/solution.py
@@ -92,8 +92,19 @@
     Z = R // X
     outer, inner = row // X, lax.rem(row, X)
 
+    def partner(k):
+        if Z & (Z - 1):
+            return lax.rem(outer + k, Z)
+        at = outer
+        bit = 1
+        while bit < Z:
+            on = (k // bit) % 2 if isinstance(k, int) else lax.rem(k // bit, 2)
+            at = at + on * bit * (1 - 2 * lax.rem(outer // bit, 2))
+            bit *= 2
+        return at
+
     def place(k, m):
-        return lax.rem(outer + k, Z) * X + lax.rem(inner + m, X)
+        return partner(k) * X + lax.rem(inner + m, X)
 
     def send(src, dst, ssem, rsem, device):
         copy = pltpu.make_async_remote_copy(

time: 77 us -> 71.9 us (0.934)
  Pallas kernels: 72.4 us -> 67.3 us
    pallas_call x1, Pallas kernels: 72.4 us -> 67.3 us  [shards(): pl.pallas_call(functools.partial(kernel, R, C), out_shape=(jax.ShapeDtype...]
where the time goes in v3:
time: 71.9 us; the launch traced here: 71.7 us
  Pallas kernels  67.3 us (94%)
  local copies, waits for them, and re-layouts  3.67 us (5%)
    pallas_call x1, Pallas kernels, shards(): pl.pallas_call(functools.partial(kernel, R, C), out_shape=(jax.ShapeDtype...  67.3 us
    unnamed x14, local copies, waits for them, and re-layouts  2.93 us

profile of v3, /device:TPU:0, one launch (start us, length us, event | category | flops | bytes accessed | tf_op | source)
XLA Modules:
  0.0 71.7 jit_solution(4366327068413305296)
XLA Ops:
  0.6 0.0 copy-start.2
  0.6 0.0 copy-start.3
  0.7 0.0 copy-start.4
  0.7 0.0 copy-start.5
  0.7 0.7 %reshape.20.lb_ref = f32[8,512]{1,0:T(8,128)S(1)} reshape(f32[4096]{0:T(1024)} %param.10) | data formatting | bytes 32768 | tf_op jit(solution)/shard_map/reshape | solution.py:461
  1.4 0.0 copy-done.2
  1.4 0.0 copy-done.3
  1.4 0.0 copy-done.4
  1.4 0.0 copy-done.5
  1.4 0.0 copy-start
  1.4 0.9 %copy-done = f32[64,512]{1,0:T(8,128)S(1)} copy-done((f32[64,512]{1,0:T(8,128)S(1)}, f32[64,512]{1,0:T(8,128)}, u32[]{:S(2)}) %copy-start) | copy-done | bytes 131096
  2.3 0.0 copy-start.1
  2.3 0.8 %copy-done.1 = f32[64,256]{1,0:T(8,128)S(1)} copy-done((f32[64,256]{1,0:T(8,128)S(1)}, f32[64,256]{1,0:T(8,128)}, u32[]{:S(2)}) %copy-start.1) | copy-done | bytes 65560
  3.2 67.3 %shard_map.86 = (f32[1,1024]{1,0:T(1,128)S(1)}, f32[1,512]{1,0:T(1,128)S(1)}) custom-call(f32[64,256]{1,0:T(8,128)S(1)} %copy-done.1, f32[64,512]{1,0:T(8,128)S(1)} %copy-done, f32[1,1024]{1,0:T(1,128)S(1)} %bitcast.4, f32[8,512]{1,0:T(8,128)S(1)} %reshape.20.lb_ref, f32[1,512]{1,0:T(1,128)S(1)} %bitcast.6, f32[4,512]{1,0:T(4,128)S(1)} %copy-done.2, ...), custom_call_target="tpu_custom_call" | custom-call | tf_op jit(solution)/shard_map/pallas_call | solution.py:425
  70.5 0.6 copy.11
  71.1 0.6 copy.12
Async XLA Ops:
  0.6 0.8 %copy-start.2 = (f32[4,512]{1,0:T(4,128)S(1)}, f32[4,512]{1,0:T(4,128)}, u32[]{:S(2)}) copy-start(f32[4,512]{1,0:T(4,128)} %hg_ref.1) | copy-start | bytes 24580
  0.6 0.8 %copy-start.3 = (f32[4,512]{1,0:T(4,128)S(1)}, f32[4,512]{1,0:T(4,128)}, u32[]{:S(2)}) copy-start(f32[4,512]{1,0:T(4,128)} %hm_ref.1) | copy-start | bytes 24580
  0.7 0.8 %copy-start.4 = (f32[1024]{0:T(1024)S(1)}, f32[1024]{0:T(1024)}, u32[]{:S(2)}) copy-start(f32[1024]{0:T(1024)} %param.9) | copy-start | bytes 12292
  0.7 0.8 %copy-start.5 = (f32[512]{0:T(512)S(1)}, f32[512]{0:T(512)}, u32[]{:S(2)}) copy-start(f32[512]{0:T(512)} %param.11) | copy-start | bytes 6148
  1.4 0.9 %copy-start = (f32[64,512]{1,0:T(8,128)S(1)}, f32[64,512]{1,0:T(8,128)}, u32[]{:S(2)}) copy-start(f32[64,512]{1,0:T(8,128)} %tgt_ref.1) | copy-start | bytes 393220
  2.3 0.8 %copy-start.1 = (f32[64,256]{1,0:T(8,128)S(1)}, f32[64,256]{1,0:T(8,128)}, u32[]{:S(2)}) copy-start(f32[64,256]{1,0:T(8,128)} %src_ref.1) | copy-start | bytes 196612
